TPU v7x, 256 devices: a whole 4x4x8 slice. The times are simulated.
256 devices in a mesh: dp: 16 (over y, x), shard: 16 (over z, core).
Axes of the slice: x: 4, y: 4, z: 8, core: 2. Of those that a mesh axis runs over, the one named last changes fastest.
Arguments:
- gradients: bfloat16 [16, 12288, 2048], P('dp', 'shard'), may hold values from -4000 to 4000, as said below
- master_weights: float32 [12288, 2048], P(('shard', 'dp')), may hold values from -6 to 6
- first_moment: float32 [12288, 2048], P(('shard', 'dp')), may hold values from -4 to 4
- second_moment: float32 [12288, 2048], P(('shard', 'dp')), may hold values from 0.05 to 2
Outputs:
- parameters: bfloat16 [12288, 2048], P('shard')
- new_master: float32 [12288, 2048], P(('shard', 'dp'))
- new_first: float32 [12288, 2048], P(('shard', 'dp'))
- new_second: float32 [12288, 2048], P(('shard', 'dp'))
Inputs may be any that keep to these rules, and one draw needn't show every extreme that they name: `gradients`: each replica's partial gradient.
All inputs are finite; a program needn't handle non-finite values.
Results may differ from a plain program's by a relative error of at most 0.006.
Values may be sent and summed in bfloat16 or wider, within the bound.
A program may use at most 64 MiB of HBM per device.

v0:
```python
import math

import jax
import jax.numpy as jnp
from jax import lax
from jax.sharding import Mesh
from jax.sharding import PartitionSpec as P

DP = ("dp_0", "dp_1")
SHARD = ("shard_0", "shard_1")
SHARD_DP = ("shard_0", "shard_1", "dp_0", "dp_1")


first_bias = 1.0 - math.exp(100.0 * math.log(0.9))
second_bias = 1.0 - math.exp(100.0 * math.log(0.95))


def split_up(array, dim, size):
    lengths = array.shape
    pieces = array.reshape(*lengths[:dim], size, lengths[dim] // size, *lengths[dim + 1 :])
    return jnp.moveaxis(pieces, dim, 0)


def sent_and_summed(array, axis, dim):
    pieces = split_up(array, dim, lax.axis_size(axis))
    arrived = lax.all_to_all(pieces, axis, split_axis=0, concat_axis=0, tiled=True)
    return arrived.astype(jnp.float32).sum(axis=0)


def sent_to_all(array, axis):
    size = lax.axis_size(axis)
    return lax.all_to_all(
        jnp.broadcast_to(array[None], (size, *array.shape)), axis, 0, 0, tiled=True
    )


def of_everyone(array, axis):
    everything = sent_to_all(array, axis)
    return jnp.sum(everything, axis=0)


def one_axis_at_a_time(array, axes):
    far, near = axes
    nearer = of_everyone(array, near)
    return of_everyone(nearer, far)


def in_order(pieces, dim):
    lengths = list(pieces.shape[1:])
    lengths[dim] *= pieces.shape[0]
    return jnp.moveaxis(pieces, 0, dim).reshape(lengths)


def gathered_copies(array, axis, dim):
    pieces = sent_to_all(array, axis)
    return in_order(pieces, dim)


def adam_update(summed, factor, master_weights, first_moment, second_moment):
    clipped = factor * summed
    new_first = 0.9 * first_moment + 0.1 * clipped
    new_second = 0.95 * second_moment + 0.05 * clipped * clipped
    first_hat = new_first / first_bias
    second_hat = new_second / second_bias
    new_master = master_weights - 0.01 * (
        first_hat / (jnp.sqrt(second_hat) + 1e-08) + 0.1 * master_weights
    )
    return (new_master, new_first, new_second)


def per_device(gradients, master_weights, first_moment, second_moment):
    rows_dev = master_weights.shape[0]
    width = master_weights.shape[1]
    entries = rows_dev * lax.axis_size(DP) * lax.axis_size(SHARD) * width
    local_grad = gradients[0].astype(jnp.float32)
    summed = sent_and_summed(local_grad.astype(jnp.bfloat16), DP, 0)
    square_sum = one_axis_at_a_time(
        jnp.sum(summed * summed), ("dp_0", ("dp_1", "shard_0", "shard_1"))
    )
    limit = 0.5 * math.sqrt(entries)
    factor = jnp.minimum(1.0, limit / jnp.sqrt(square_sum + 1e-06))
    new_master, new_first, new_second = adam_update(
        summed, factor, master_weights, first_moment, second_moment
    )
    owned_params = new_master.astype(jnp.bfloat16)
    parameters = gathered_copies(owned_params, DP, 0)
    return (parameters, new_master, new_first, new_second)


def solution(mesh):
    split = Mesh(mesh.devices.reshape(4, 4, 8, 2), ("dp_0", "dp_1", "shard_0", "shard_1"))
    return jax.shard_map(
        per_device,
        mesh=split,
        in_specs=(P(DP, SHARD, None), P(SHARD_DP, None), P(SHARD_DP, None), P(SHARD_DP, None)),
        out_specs=(P(SHARD, None), P(SHARD_DP, None), P(SHARD_DP, None), P(SHARD_DP, None)),
        check_vma=False,
    )
```

profile of v0, /device:TPU:1, one launch (start us, length us, event | category | flops | bytes accessed | tf_op | source)
XLA Modules:
  0.0 123.0 jit_solution(8021457390038427170)
XLA Ops:
  0.6 46.1 %all_to_all.22 = bf16[16,48,2048]{2,1,0:T(8,128)(2,1)S(1)} all-to-all(bf16[16,48,2048]{2,1,0:T(8,128)(2,1)} %bitcast.3), channel_id=1, replica_groups=mesh['dp_0'=4,'dp_1'=4,'shard_0'=8,'shard_1'=2] {'dp_0','dp_1'}, dimensions={0} | all-to-all | bytes 6291456 | tf_op jit(solution)/shard_map/all_to_all | solution.py:26
  46.7 0.0 copy-start
  46.7 0.0 copy-start.1
  46.7 0.0 copy-start.2
  46.7 0.6 convert_reduce_fusion
  47.3 0.7 multiply_reduce_fusion
  48.0 0.7 broadcast_in_dim.6
  48.7 20.4 %all_to_all.23 = f32[64,1,1]{2,1,0:T(1,128)S(1)} all-to-all(f32[64,1,1]{2,1,0:T(1,128)S(1)} %broadcast_in_dim.6), channel_id=1, replica_groups=mesh['dp_0'=4,'dp_1'=4,'shard_0'=8,'shard_1'=2] {'dp_1','shard_0','shard..., dimensions={0} | all-to-all | bytes 512 | tf_op jit(solution)/shard_map/all_to_all | solution.py:32
  69.2 0.7 reduce_sum.38
  69.8 0.6 broadcast_in_dim.7
  70.5 6.5 %all_to_all.24 = f32[4,1,1]{2,1,0:T(1,128)S(1)} all-to-all(f32[4,1,1]{2,1,0:T(1,128)S(1)} %broadcast_in_dim.7), channel_id=1, replica_groups=mesh['dp_0'=4,'dp_1'=4,'shard_0'=8,'shard_1'=2] {'dp_0'}, dimensions={0} | all-to-all | bytes 32 | tf_op jit(solution)/shard_map/all_to_all | solution.py:32
  77.0 0.6 reduce_sum.39
  78.2 0.0 copy-done
  78.3 0.0 copy-done.1
  78.3 0.0 copy-done.2
  78.3 1.2 fusion.1
  79.5 0.4 broadcast_in_dim.8
  79.9 41.5 %all_to_all.25 = bf16[16,48,2048]{2,1,0:T(8,128)(2,1)S(1)} all-to-all(bf16[16,48,2048]{2,1,0:T(8,128)(2,1)S(1)} %broadcast_in_dim.8), channel_id=1, replica_groups=mesh['dp_0'=4,'dp_1'=4,'shard_0'=8,'shard_1'=2] {'dp_0','dp_1'}, dimensions={0} | all-to-all | bytes 6291456 | tf_op jit(solution)/shard_map/all_to_all | solution.py:32
  121.4 1.7 %copy.13 = bf16[768,2048]{1,0:T(8,128)(2,1)} copy(bf16[768,2048]{1,0:T(8,128)(2,1)S(1)} %bitcast.2) | data formatting | bytes 6291456
Async XLA Ops:
  46.7 31.5 %copy-start = (f32[48,2048]{1,0:T(8,128)S(1)}, f32[48,2048]{1,0:T(8,128)}, u32[]{:S(2)}) copy-start(f32[48,2048]{1,0:T(8,128)} %param.5) | copy-start | bytes 1179652
  46.7 31.5 %copy-start.1 = (f32[48,2048]{1,0:T(8,128)S(1)}, f32[48,2048]{1,0:T(8,128)}, u32[]{:S(2)}) copy-start(f32[48,2048]{1,0:T(8,128)} %param.6) | copy-start | bytes 1179652
  46.7 31.5 %copy-start.2 = (f32[48,2048]{1,0:T(8,128)S(1)}, f32[48,2048]{1,0:T(8,128)}, u32[]{:S(2)}) copy-start(f32[48,2048]{1,0:T(8,128)} %param.7) | copy-start | bytes 1179652
where the time goes:
time: 125 us; the launch traced here: 123 us
  blocking collectives  115 us (92%)
  other arithmetic  3.77 us (3%)
  local copies, waits for them, and re-layouts  3.36 us (3%)
  between operations  1.38 us (1%)
    all_to_all x3, blocking collectives, sent_to_all(): lax.all_to_all(jnp.broadcast_to(array[None], (size, *array.shape)), axis,...  68.4 us
    all_to_all x1, blocking collectives, sent_and_summed(): lax.all_to_all(pieces, axis, split_axis=0, concat_axis=0, tiled=True)  46.1 us

commit v1 on v0

v1 whole, which is shorter than its diff:
```python
import math

import jax
import jax.numpy as jnp
from jax import lax
from jax.experimental import pallas as pl
from jax.experimental.pallas import tpu as pltpu
from jax.sharding import Mesh
from jax.sharding import PartitionSpec as P

DP = ("y", "x")
SHARD = ("z", "core")
SHARD_DP = ("z", "core", "y", "x")
MESH = pl.DeviceIdType.MESH

first_bias = 1.0 - math.exp(100.0 * math.log(0.9))
second_bias = 1.0 - math.exp(100.0 * math.log(0.95))

F32 = jnp.float32
BF16 = jnp.bfloat16


class Copies:
    def __init__(self, send_sems, recv_sems):
        self.send_sems, self.recv_sems = send_sems, recv_sems
        self.made = {}

    def start(self, key, src, dst, device):
        at = len(self.made)
        copy = pltpu.make_async_remote_copy(
            src_ref=src,
            dst_ref=dst,
            send_sem=self.send_sems.at[at],
            recv_sem=self.recv_sems.at[at],
            device_id=device,
            device_id_type=MESH,
        )
        copy.start()
        self.made[key] = copy

    def arrived(self, key):
        self.made[key].wait_recv()

    def all_sent(self):
        for copy in self.made.values():
            copy.wait_send()


N_COPIES = 60 + 44 + 30


def kernel(
    entries,
    g_hbm, w_hbm, m_hbm, v_hbm,
    params, w_out, m_out, v_out,
    gv, r1, d1, x1, tf, tb, r2, d2, x2, w, m, v, np_, nz,
    load_sems, send_sems, recv_sems, gossip,
):
    ix, iy = lax.axis_index("x"), lax.axis_index("y")
    iz, ic = lax.axis_index("z"), lax.axis_index("core")
    nz_ring = lax.axis_size("z")
    n_core = lax.axis_size("core")
    half = g_hbm.shape[3] // 2
    quarter = half // 2

    def up(i, by, n=4):
        return lax.rem(i + by, n)

    first_axis, second_axis = ("x", "y"), ("y", "x")
    a = (ix, iy)
    b = (iy, ix)
    step_of = (1, 3)
    group_by = (2, 1, 3, 0)
    cols_of = (pl.ds(0, quarter), pl.ds(quarter, quarter))

    def at_block(ref, h, ai, bi, cols):
        y, x = (bi, ai) if h == 0 else (ai, bi)
        return ref.at[y, x, :, cols]

    def near(axis, i, direction):
        return {axis: up(i, step_of[direction])}

    loads = {}

    def load(key, src, dst):
        copy = pltpu.make_async_copy(src, dst, load_sems.at[len(loads)])
        copy.start()
        loads[key] = copy

    for k in range(4):
        for h in range(2):
            bi = up(b[h], group_by[k])
            cols = pl.ds(h * half, half)
            src = g_hbm.at[bi, :, :, cols] if h == 0 else g_hbm.at[:, bi, :, cols]
            load((h, k), src, gv.at[h, k])
    load("w", w_hbm, w)
    load("m", m_hbm, m)
    load("v", v_hbm, v)

    barrier = pltpu.get_barrier_semaphore()
    neighbours = [{"x": up(ix, s)} for s in step_of] + [{"y": up(iy, s)} for s in step_of]
    neighbours += [{"z": up(iz, s, nz_ring)} for s in (1, nz_ring - 1)]
    neighbours += [{"core": up(ic, s, n_core)} for s in range(1, n_core)]
    for device in neighbours:
        pl.semaphore_signal(barrier, inc=1, device_id=device, device_id_type=MESH)
    pl.semaphore_wait(barrier, len(neighbours))

    rounds = nz_ring // 2

    def tell(r):
        for side, s in enumerate((1, nz_ring - 1)):
            pl.semaphore_signal(
                gossip.at[r, side], inc=1,
                device_id={"z": up(iz, s, nz_ring)}, device_id_type=MESH,
            )

    def told(r):
        for side in range(2):
            pl.semaphore_wait(gossip.at[r, side], 1)

    copies = Copies(send_sems, recv_sems)

    def send_own(k):
        for h in range(2):
            loads[h, k].wait()
            for direction in range(2):
                relayed, other = cols_of[direction], cols_of[1 - direction]
                device = near(first_axis[h], a[h], direction)
                copies.start(
                    ("r1", h, direction, k),
                    gv.at[h, k, up(a[h], 2), :, relayed],
                    r1.at[h, direction, k],
                    device,
                )
            for direction in range(2):
                relayed, other = cols_of[direction], cols_of[1 - direction]
                device = near(first_axis[h], a[h], direction)
                target = up(a[h], step_of[direction])
                copies.start(
                    ("d1o", h, direction, k),
                    gv.at[h, k, target, :, other],
                    d1.at[h, direction, k, :, other],
                    device,
                )

    def relay(k):
        for h in range(2):
            for direction in range(2):
                relayed = cols_of[direction]
                target = up(a[h], step_of[direction])
                copies.arrived(("r1", h, direction, k))
                x1[h, direction, k] = (
                    gv[h, k, target, :, relayed].astype(F32)
                    + r1[h, direction, k].astype(F32)
                ).astype(BF16)
                copies.start(
                    ("d1r", h, direction, k),
                    x1.at[h, direction, k],
                    d1.at[h, direction, k, :, relayed],
                    near(first_axis[h], a[h], direction),
                )

    def complete(k):
        for h in range(2):
            for direction in range(2):
                copies.arrived(("d1o", h, direction, k))
                copies.arrived(("d1r", h, direction, k))
            total = (
                gv[h, k, a[h]].astype(F32)
                + d1[h, 0, k].astype(F32)
                + d1[h, 1, k].astype(F32)
            )
            tf[h, k] = total
            if k < 3:
                tb[h, k] = total.astype(BF16)
            if k == 0:
                for direction in range(2):
                    relayed = cols_of[direction]
                    copies.start(
                        ("r2", h, direction),
                        tb.at[h, 0, :, relayed],
                        r2.at[h, direction],
                        near(second_axis[h], b[h], direction),
                    )
            if k in (1, 2):
                direction = k - 1
                other = cols_of[1 - direction]
                copies.start(
                    ("d2o", h, direction),
                    tb.at[h, k, :, other],
                    d2.at[h, direction, :, other],
                    near(second_axis[h], b[h], direction),
                )

    def relay_second(k):
        direction = k - 1
        relayed = cols_of[direction]
        for h in range(2):
            copies.arrived(("r2", h, direction))
            x2[h, direction] = (
                tf[h, k, :, relayed] + r2[h, direction].astype(F32)
            ).astype(BF16)
            copies.start(
                ("d2r", h, direction),
                x2.at[h, direction],
                d2.at[h, direction, :, relayed],
                near(second_axis[h], b[h], direction),
            )

    send_own(0)
    tell(0)
    send_own(1)
    relay(0)
    told(0)
    tell(1)
    send_own(2)
    relay(1)
    complete(0)
    told(1)
    tell(2)
    send_own(3)
    relay(2)
    complete(1)
    told(2)
    tell(3)
    relay_second(1)
    relay(3)
    complete(2)
    relay_second(2)
    complete(3)
    told(3)

    part = jnp.zeros((8, half), F32)
    for h in range(2):
        for direction in range(2):
            copies.arrived(("d2o", h, direction))
            copies.arrived(("d2r", h, direction))
        total = tf[h, 3] + d2[h, 0].astype(F32) + d2[h, 1].astype(F32)
        tf[h, 3] = total
        square = total * total
        part = part + jnp.sum(square.reshape(-1, 8, half), axis=0)
    row = jnp.sum(part, axis=0, keepdims=True)
    lanes = row[:, 0:128]
    for c in range(1, half // 128):
        lanes = lanes + row[:, c * 128 : (c + 1) * 128]

    np_[0] = lanes
    for i in range(1, 16):
        device = {"y": up(iy, i // 4), "x": up(ix, i % 4)}
        copies.start(("np", i), np_.at[0], np_.at[i], device)
    loads["w"].wait()
    loads["m"].wait()
    loads["v"].wait()
    for i in range(1, 16):
        copies.arrived(("np", i))
    nz[0] = jnp.sum(np_[...], axis=0)
    others = nz_ring * n_core
    for i in range(1, others):
        device = {"z": up(iz, i // n_core, nz_ring), "core": up(ic, i % n_core, n_core)}
        copies.start(("nz", i), nz.at[0], nz.at[i], device)
    for i in range(1, others):
        copies.arrived(("nz", i))
    square_sum = jnp.sum(jnp.sum(nz[...], axis=0), axis=1, keepdims=True)
    limit = 0.5 * math.sqrt(entries)
    factor = jnp.minimum(1.0, limit / jnp.sqrt(square_sum + 1e-06))

    def update(h):
        cols = pl.ds(h * half, half)
        clipped = factor * tf[h, 3]
        new_first = 0.9 * m[:, cols] + 0.1 * clipped
        new_second = 0.95 * v[:, cols] + 0.05 * clipped * clipped
        first_hat = new_first / first_bias
        second_hat = new_second / second_bias
        master = w[:, cols]
        new_master = master - 0.01 * (
            first_hat / (jnp.sqrt(second_hat) + 1e-08) + 0.1 * master
        )
        params[iy, ix, :, cols] = new_master.astype(BF16)
        w_out[:, cols] = new_master
        m_out[:, cols] = new_first
        v_out[:, cols] = new_second

    def columns(h, side=None):
        if side is None:
            return pl.ds(h * half, half)
        return pl.ds(h * half + side * quarter, quarter)

    def along_second(h, direction):
        piece = at_block(params, h, a[h], b[h], columns(h))
        copies.start(("g2", h, direction), piece, piece, near(second_axis[h], b[h], direction))

    def forward_second(h, direction):
        came_from = up(b[h], step_of[1 - direction])
        copies.arrived(("g2", h, direction))
        piece = at_block(params, h, a[h], came_from, columns(h, direction))
        copies.start(("f2", h, direction), piece, piece, near(second_axis[h], b[h], direction))

    def along_first(h, j, side=None):
        bi = up(b[h], (0, 3, 1, 2)[j])
        piece = at_block(params, h, a[h], bi, columns(h, side))
        for direction in range(2):
            copies.start(
                ("g1", h, direction, j, side), piece, piece,
                near(first_axis[h], a[h], direction),
            )

    def forward_first(h, j):
        bi = up(b[h], (0, 3, 1, 2)[j])
        for direction in range(2):
            side = direction if j == 3 else None
            copies.arrived(("g1", h, direction, j, side))
            came_from = up(a[h], step_of[1 - direction])
            piece = at_block(params, h, came_from, bi, columns(h, direction))
            copies.start(
                ("f1", h, direction, j), piece, piece,
                near(first_axis[h], a[h], direction),
            )

    for h in range(2):
        update(h)
        for direction in range(2):
            along_second(h, direction)
    for h in range(2):
        along_first(h, 0)
    for j in (1, 2):
        for h in range(2):
            forward_second(h, j - 1)
            along_first(h, j)
    for h in range(2):
        forward_first(h, 0)
    for direction in range(2):
        for h in range(2):
            copies.arrived(("f2", h, direction))
            along_first(h, 3, direction)
    for j in (1, 2, 3):
        for h in range(2):
            forward_first(h, j)
    for h in range(2):
        for direction in range(2):
            copies.arrived(("g1", h, direction, 3, 1 - direction))
            for j in range(4):
                copies.arrived(("f1", h, direction, j))
    copies.all_sent()


def per_device(gradients, master_weights, first_moment, second_moment):
    rows, width = master_weights.shape
    entries = rows * lax.axis_size(DP) * lax.axis_size(SHARD) * width
    half, quarter = width // 2, width // 4
    grads = gradients.reshape(4, 4, rows, width)
    owned = jax.ShapeDtypeStruct((rows, width), F32)
    hbm = pl.BlockSpec(memory_space=pltpu.HBM)
    vmem = pl.BlockSpec(memory_space=pltpu.VMEM)
    peers = lax.axis_size("z") * lax.axis_size("core")
    parameters, new_master, new_first, new_second = pl.pallas_call(
        lambda *refs: kernel(entries, *refs),
        out_shape=(jax.ShapeDtypeStruct((4, 4, rows, width), BF16), owned, owned, owned),
        in_specs=[hbm] * 4,
        out_specs=(vmem,) * 4,
        scratch_shapes=[
            pltpu.VMEM((2, 4, 4, rows, half), BF16),
            pltpu.VMEM((2, 2, 4, rows, quarter), BF16),
            pltpu.VMEM((2, 2, 4, rows, half), BF16),
            pltpu.VMEM((2, 2, 4, rows, quarter), BF16),
            pltpu.VMEM((2, 4, rows, half), F32),
            pltpu.VMEM((2, 3, rows, half), BF16),
            pltpu.VMEM((2, 2, rows, quarter), BF16),
            pltpu.VMEM((2, 2, rows, half), BF16),
            pltpu.VMEM((2, 2, rows, quarter), BF16),
            pltpu.VMEM((rows, width), F32),
            pltpu.VMEM((rows, width), F32),
            pltpu.VMEM((rows, width), F32),
            pltpu.VMEM((16, 1, 128), F32),
            pltpu.VMEM((peers, 1, 128), F32),
            pltpu.SemaphoreType.DMA((11,)),
            pltpu.SemaphoreType.DMA((N_COPIES,)),
            pltpu.SemaphoreType.DMA((N_COPIES,)),
            pltpu.SemaphoreType.REGULAR((lax.axis_size("z") // 2, 2)),
        ],
        compiler_params=pltpu.CompilerParams(collective_id=0, has_side_effects=True),
    )(grads, master_weights, first_moment, second_moment)
    return (parameters.reshape(16 * rows, width), new_master, new_first, new_second)


def solution(mesh):
    split = Mesh(mesh.devices.reshape(4, 4, 8, 2), ("y", "x", "z", "core"))
    return jax.shard_map(
        per_device,
        mesh=split,
        in_specs=(P(DP, SHARD, None), P(SHARD_DP, None), P(SHARD_DP, None), P(SHARD_DP, None)),
        out_specs=(P(SHARD, None), P(SHARD_DP, None), P(SHARD_DP, None), P(SHARD_DP, None)),
        check_vma=False,
    )
```

time: 125 us -> 68.9 us (0.55)
  blocking collectives: 115 us -> 0 us
  Pallas kernels: 0 us -> 61.2 us
  other arithmetic: 3.77 us -> 0 us
  local copies, waits for them, and re-layouts: 3.36 us -> 6.31 us
    all_to_all x4 -> x0, blocking collectives: 115 us -> none  [the longest x3 68.4 us: sent_to_all(): lax.all_to_all(jnp.broadcast_to(array[None], (size, *array.shape)), axis,...]
    pallas_call x0 -> x1, Pallas kernels: none -> 61.2 us  [per_device(): pl.pallas_call(lambda *refs: kernel(entries, *refs), out_shape=(jax.Shape...]
    unnamed x7 -> x10, local copies, waits for them, and re-layouts: 1.68 us -> 6.31 us
    reduce_sum x4 -> x0, other arithmetic: 2.57 us -> none  [the longest x2 1.27 us: of_everyone(): return jnp.sum(everything, axis=0)]
    broadcast_in_dim x3 -> x0, local copies, waits for them, and re-layouts: 1.68 us -> none  [sent_to_all(): jnp.broadcast_to(array[None], (size, *array.shape))]
where the time goes in v1:
time: 68.9 us; the launch traced here: 68.1 us
  Pallas kernels  61.2 us (89%)
  local copies, waits for them, and re-layouts  6.31 us (9%)
    pallas_call x1, Pallas kernels, per_device(): pl.pallas_call(lambda *refs: kernel(entries, *refs), out_shape=(jax.Shape...  61.2 us
    unnamed x10, local copies, waits for them, and re-layouts  6.31 us

profile of v1, /device:TPU:1, one launch (start us, length us, event | category | flops | bytes accessed | tf_op | source)
XLA Modules:
  0.0 68.1 jit_solution(13019436028753861743)
XLA Ops:
  0.6 61.2 %shard_map.75 = (bf16[4,4,48,2048]{3,2,1,0:T(8,128)(2,1)}, f32[48,2048]{1,0:T(8,128)}, f32[48,2048]{1,0:T(8,128)}, f32[48,2048]{1,0:T(8,128)}) custom-call(bf16[4,4,48,2048]{3,2,1,0:T(8,128)(2,1)} %bitcast.3, f32[48,2048]{1,0:T(8,128)} %refs_1_.1, f32[48,2048]{1,0:T(8,128)} %refs_2_.1, f32[48,2048]{1,0:T(8,128)} %refs_3_.1), custom_call_target="tpu_custom_call" | custom-call | tf_op jit(solution)/shard_map/pallas_call | solution.py:355
  61.8 0.0 copy-start.2
  61.8 0.0 copy-start.1
  61.8 0.0 copy-start
  61.8 4.1 %copy.12 = bf16[768,2048]{1,0:T(8,128)(2,1)} copy(bf16[768,2048]{1,0:T(8,128)(2,1)} %bitcast.2) | data formatting | bytes 6291456
  65.9 0.0 copy-done.2
  65.9 0.7 %copy.13 = f32[48,2048]{1,0:T(8,128)} copy(f32[48,2048]{1,0:T(8,128)S(1)} %copy-done.2) | data formatting | bytes 786432
  66.6 0.0 copy-done.1
  66.6 0.7 %copy.14 = f32[48,2048]{1,0:T(8,128)} copy(f32[48,2048]{1,0:T(8,128)S(1)} %copy-done.1) | data formatting | bytes 786432
  67.4 0.0 copy-done
  67.4 0.7 %copy.15 = f32[48,2048]{1,0:T(8,128)} copy(f32[48,2048]{1,0:T(8,128)S(1)} %copy-done) | data formatting | bytes 786432
Async XLA Ops:
  61.8 4.1 %copy-start.2 = (f32[48,2048]{1,0:T(8,128)S(1)}, f32[48,2048]{1,0:T(8,128)}, u32[]{:S(2)}) copy-start(f32[48,2048]{1,0:T(8,128)} %get-tuple-element.17) | copy-start | bytes 1179652
  61.8 4.8 %copy-start.1 = (f32[48,2048]{1,0:T(8,128)S(1)}, f32[48,2048]{1,0:T(8,128)}, u32[]{:S(2)}) copy-start(f32[48,2048]{1,0:T(8,128)} %get-tuple-element.18) | copy-start | bytes 1179652
  61.8 5.6 %copy-start = (f32[48,2048]{1,0:T(8,128)S(1)}, f32[48,2048]{1,0:T(8,128)}, u32[]{:S(2)}) copy-start(f32[48,2048]{1,0:T(8,128)} %get-tuple-element.19) | copy-start | bytes 1179652

commit v2 on v1

--- a/solution.py
+++ b/solution.py
@@ -45,6 +45,8 @@
         for copy in self.made.values():
             copy.wait_send()
 
+
+VMEM_LIMIT = 59 * 2**20
 
 N_COPIES = 60 + 44 + 30
 
@@ -348,13 +350,13 @@
     entries = rows * lax.axis_size(DP) * lax.axis_size(SHARD) * width
     half, quarter = width // 2, width // 4
     grads = gradients.reshape(4, 4, rows, width)
-    owned = jax.ShapeDtypeStruct((rows, width), F32)
+    owned = pltpu.VMEM((rows, width), F32)
     hbm = pl.BlockSpec(memory_space=pltpu.HBM)
     vmem = pl.BlockSpec(memory_space=pltpu.VMEM)
     peers = lax.axis_size("z") * lax.axis_size("core")
     parameters, new_master, new_first, new_second = pl.pallas_call(
         lambda *refs: kernel(entries, *refs),
-        out_shape=(jax.ShapeDtypeStruct((4, 4, rows, width), BF16), owned, owned, owned),
+        out_shape=(pltpu.VMEM((4, 4, rows, width), BF16), owned, owned, owned),
         in_specs=[hbm] * 4,
         out_specs=(vmem,) * 4,
         scratch_shapes=[
@@ -377,7 +379,9 @@
             pltpu.SemaphoreType.DMA((N_COPIES,)),
             pltpu.SemaphoreType.REGULAR((lax.axis_size("z") // 2, 2)),
         ],
-        compiler_params=pltpu.CompilerParams(collective_id=0, has_side_effects=True),
+        compiler_params=pltpu.CompilerParams(
+            collective_id=0, has_side_effects=True, vmem_limit_bytes=VMEM_LIMIT
+        ),
     )(grads, master_weights, first_moment, second_moment)
     return (parameters.reshape(16 * rows, width), new_master, new_first, new_second)
 

time: 68.9 us -> 64.4 us (0.935)
  local copies, waits for them, and re-layouts: 6.31 us -> 3.9 us
  Pallas kernels: 61.2 us -> 59.2 us
    unnamed x10 -> x4, local copies, waits for them, and re-layouts: 6.31 us -> 3.9 us
    pallas_call x1, Pallas kernels: 61.2 us -> 59.2 us  [per_device(): pl.pallas_call(lambda *refs: kernel(entries, *refs), out_shape=(pltpu.VME...]
where the time goes in v2:
time: 64.4 us; the launch traced here: 63.7 us
  Pallas kernels  59.2 us (92%)
  local copies, waits for them, and re-layouts  3.9 us (6%)
    pallas_call x1, Pallas kernels, per_device(): pl.pallas_call(lambda *refs: kernel(entries, *refs), out_shape=(pltpu.VME...  59.2 us
    unnamed x4, local copies, waits for them, and re-layouts  3.9 us

profile of v2, /device:TPU:1, one launch (start us, length us, event | category | flops | bytes accessed | tf_op | source)
XLA Modules:
  0.0 63.7 jit_solution(4960127594970998154)
XLA Ops:
  0.6 59.2 %shard_map.75 = (bf16[4,4,48,2048]{3,2,1,0:T(8,128)(2,1)S(1)}, f32[48,2048]{1,0:T(8,128)S(1)}, f32[48,2048]{1,0:T(8,128)S(1)}, f32[48,2048]{1,0:T(8,128)S(1)}) custom-call(bf16[4,4,48,2048]{3,2,1,0:T(8,128)(2,1)} %bitcast.3, f32[48,2048]{1,0:T(8,128)} %refs_1_.1, f32[48,2048]{1,0:T(8,128)} %refs_2_.1, f32[48,2048]{1,0:T(8,128)} %refs_3_.1), custom_call_target="tpu_custom_call" | custom-call | tf_op jit(solution)/shard_map/pallas_call | solution.py:357
  59.8 1.7 %copy.12 = bf16[768,2048]{1,0:T(8,128)(2,1)} copy(bf16[768,2048]{1,0:T(8,128)(2,1)S(1)} %bitcast.2) | data formatting | bytes 6291456
  61.5 0.7 %copy.13 = f32[48,2048]{1,0:T(8,128)} copy(f32[48,2048]{1,0:T(8,128)S(1)} %get-tuple-element.13) | data formatting | bytes 786432
  62.2 0.7 %copy.14 = f32[48,2048]{1,0:T(8,128)} copy(f32[48,2048]{1,0:T(8,128)S(1)} %get-tuple-element.14) | data formatting | bytes 786432
  63.0 0.7 %copy.15 = f32[48,2048]{1,0:T(8,128)} copy(f32[48,2048]{1,0:T(8,128)S(1)} %get-tuple-element.15) | data formatting | bytes 786432

commit v3 on v0

v3 whole, which is shorter than its diff:
```python
import math

import jax
import jax.numpy as jnp
from jax import lax
from jax.experimental import pallas as pl
from jax.experimental.pallas import tpu as pltpu
from jax.sharding import Mesh
from jax.sharding import PartitionSpec as P

DP = ("y", "x")
SHARD = ("z", "core")
SHARD_DP = ("z", "core", "y", "x")
MESH = pl.DeviceIdType.MESH

first_bias = 1.0 - math.exp(100.0 * math.log(0.9))
second_bias = 1.0 - math.exp(100.0 * math.log(0.95))

F32 = jnp.float32
BF16 = jnp.bfloat16
VMEM_LIMIT = 59 * 2**20


def table(*groups):
    keys = []
    for name, *dims in groups:
        index = [()]
        for dim in dims:
            index = [i + (j,) for i in index for j in range(dim)]
        keys += [(name, *i) for i in index]
    return {key: at for at, key in enumerate(keys)}


RECEIVED = table(
    ("r1", 2, 4), ("d1", 2, 4), ("r2", 2), ("d2", 2), ("np",), ("nz",),
    ("g2", 2, 2, 2), ("f2", 2, 2), ("g1", 2, 4, 2), ("f1",),
)
SENT = table(("rs",), ("np",), ("nz",), ("ag",))
LOADED = table(("gx", 2), ("gv", 2), ("state",))


def kernel(
    entries,
    g_hbm, w_hbm, m_hbm, v_hbm,
    params, w_out, m_out, v_out,
    gx, gv, land, x1, tf, tb, x2, state, np_, nz,
    load_sems, send_sems, recv_sems, gossip,
):
    ix, iy = lax.axis_index("x"), lax.axis_index("y")
    iz, ic = lax.axis_index("z"), lax.axis_index("core")
    z_size = lax.axis_size("z")
    n_core = lax.axis_size("core")
    half = g_hbm.shape[3] // 2
    quarter = half // 2

    def up(i, by, n=4):
        return lax.rem(i + by, n)

    first_axis, second_axis = ("x", "y"), ("y", "x")
    a = (ix, iy)
    b = (iy, ix)
    step_of = (1, 3)
    group_by = (2, 1, 3, 0)

    def r1(h, k):
        return land.at[pl.ds((h * 4 + k) * 2, 2)]

    def d1(h, k):
        return land.at[pl.ds(16 + (h * 4 + k) * 4, 4)]

    def r2(h):
        return land.at[pl.ds(48 + h * 2, 2)]

    def d2(h):
        return land.at[pl.ds(52 + h * 4, 4)]

    def whole(ref, direction):
        return jnp.concatenate(
            [ref[direction * 2].astype(F32), ref[direction * 2 + 1].astype(F32)], axis=1
        )

    def cols(h, side=None):
        if side is None:
            return pl.ds(h * half, half)
        return pl.ds(h * half + side * quarter, quarter)

    def side_cols(side):
        return pl.ds(side * quarter, quarter)

    def block(h, ai, bi):
        return (bi, ai) if h == 0 else (ai, bi)

    def near(axis, i, direction):
        return {axis: up(i, step_of[direction])}

    def along_first(h, direction):
        return near(first_axis[h], a[h], direction)

    def along_second(h, direction):
        return near(second_axis[h], b[h], direction)

    def load(key, src, dst):
        pltpu.make_async_copy(src, dst, load_sems.at[LOADED[key]]).start()

    def loaded(key, dst):
        pltpu.make_async_copy(dst, dst, load_sems.at[LOADED[key]]).wait()

    for h in range(2):
        far = up(a[h], 2)
        src = g_hbm.at[:, far, :, cols(h)] if h == 0 else g_hbm.at[far, :, :, cols(h)]
        load(("gx", h), src, gx.at[h])

    barrier = pltpu.get_barrier_semaphore()
    neighbours = [{"x": up(ix, s)} for s in step_of] + [{"y": up(iy, s)} for s in step_of]
    neighbours += [{"z": up(iz, s, z_size)} for s in (1, z_size - 1)]
    neighbours += [{"core": up(ic, s, n_core)} for s in range(1, n_core)]
    for device in neighbours:
        pl.semaphore_signal(barrier, inc=1, device_id=device, device_id_type=MESH)

    for h in range(2):
        load(("gv", h), g_hbm.at[:, :, :, cols(h)], gv.at[h])
    for i, ref in enumerate((w_hbm, m_hbm, v_hbm)):
        load(("state",), ref, state.at[i])
    pl.semaphore_wait(barrier, len(neighbours))

    def tell(r):
        for s in (1, z_size - 1):
            pl.semaphore_signal(
                gossip.at[r], inc=1,
                device_id={"z": up(iz, s, z_size)}, device_id_type=MESH,
            )

    def told(r):
        pl.semaphore_wait(gossip.at[r], 2)

    def send(sent, key, src, dst, device):
        pltpu.make_async_remote_copy(
            src_ref=src,
            dst_ref=dst,
            send_sem=send_sems.at[SENT[sent,]],
            recv_sem=recv_sems.at[RECEIVED[key]],
            device_id=device,
            device_id_type=MESH,
        ).start()

    def arrived(key, bytes_of):
        pltpu.make_async_copy(bytes_of, bytes_of, recv_sems.at[RECEIVED[key]]).wait()

    def all_sent(sent, bytes_of):
        pltpu.make_async_copy(bytes_of, bytes_of, send_sems.at[SENT[sent,]]).wait()

    def send_far(k):
        for h in range(2):
            bi = up(b[h], group_by[k])
            for direction in range(2):
                send(
                    "rs", ("r1", h, k),
                    gx.at[h, bi, :, side_cols(direction)],
                    r1(h, k).at[direction],
                    along_first(h, direction),
                )

    def send_near(k):
        for h in range(2):
            bi = up(b[h], group_by[k])
            for direction in range(2):
                other = 1 - direction
                y, x = block(h, up(a[h], step_of[direction]), bi)
                send(
                    "rs", ("d1", h, k),
                    gv.at[h, y, x, :, side_cols(other)],
                    d1(h, k).at[direction * 2 + other],
                    along_first(h, direction),
                )

    def relay(k):
        for h in range(2):
            bi = up(b[h], group_by[k])
            arrived(("r1", h, k), r1(h, k))
            for direction in range(2):
                y, x = block(h, up(a[h], step_of[direction]), bi)
                x1[h, k, direction] = (
                    gv[h, y, x, :, side_cols(direction)].astype(F32)
                    + r1(h, k)[direction].astype(F32)
                ).astype(BF16)
                send(
                    "rs", ("d1", h, k),
                    x1.at[h, k, direction],
                    d1(h, k).at[direction * 2 + direction],
                    along_first(h, direction),
                )

    def complete(k):
        for h in range(2):
            bi = up(b[h], group_by[k])
            arrived(("d1", h, k), d1(h, k))
            y, x = block(h, a[h], bi)
            total = gv[h, y, x].astype(F32) + whole(d1(h, k), 0) + whole(d1(h, k), 1)
            tf[h, k] = total
            if k < 3:
                tb[h, k] = total.astype(BF16)
            if k == 0:
                for direction in range(2):
                    send(
                        "rs", ("r2", h),
                        tb.at[h, 0, :, side_cols(direction)],
                        r2(h).at[direction],
                        along_second(h, direction),
                    )
            if k in (1, 2):
                direction = k - 1
                other = 1 - direction
                send(
                    "rs", ("d2", h),
                    tb.at[h, k, :, side_cols(other)],
                    d2(h).at[direction * 2 + other],
                    along_second(h, direction),
                )

    def relay_second():
        for h in range(2):
            arrived(("r2", h), r2(h))
            for direction in range(2):
                x2[h, direction] = (
                    tf[h, 1 + direction, :, side_cols(direction)]
                    + r2(h)[direction].astype(F32)
                ).astype(BF16)
                send(
                    "rs", ("d2", h),
                    x2.at[h, direction],
                    d2(h).at[direction * 2 + direction],
                    along_second(h, direction),
                )

    for h in range(2):
        loaded(("gx", h), gx.at[h])
    for k in range(4):
        send_far(k)
    tell(0)
    for h in range(2):
        loaded(("gv", h), gv.at[h])
    send_near(0)
    relay(0)
    told(0)
    tell(1)
    send_near(1)
    relay(1)
    relay(2)
    told(1)
    tell(2)
    send_near(2)
    complete(0)
    relay(3)
    told(2)
    tell(3)
    complete(1)
    send_near(3)
    complete(2)
    relay_second()
    complete(3)
    told(3)
    loaded(("state",), state)

    lanes = jnp.zeros((8, 128), F32)
    for h in range(2):
        arrived(("d2", h), d2(h))
        total = tf[h, 3] + whole(d2(h), 0) + whole(d2(h), 1)
        tf[h, 3] = total
        square = total * total
        by_row = jnp.sum(square.reshape(-1, 8, half), axis=0)
        for c in range(half // 128):
            lanes = lanes + by_row[:, c * 128 : (c + 1) * 128]

    np_[0] = jnp.sum(lanes, axis=0, keepdims=True)
    distance = {0: 0, 1: 1, 2: 2, 3: 1}
    plane = sorted(
        ((i, j) for i in range(4) for j in range(4)),
        key=lambda at: -distance[at[0]] - distance[at[1]],
    )[:-1]
    for i, j in plane:
        slot = i * 4 + j
        send("np", ("np",), np_.at[0], np_.at[slot], {"y": up(iy, i), "x": up(ix, j)})
    arrived(("np",), np_.at[pl.ds(1, 15)])
    nz[0] = jnp.sum(np_[...], axis=0)
    line = sorted(
        ((i, j) for i in range(z_size) for j in range(n_core)),
        key=lambda at: -min(at[0], z_size - at[0]) - 0.5 * at[1],
    )[:-1]
    for i, j in line:
        slot = i * n_core + j
        device = {"z": up(iz, i, z_size), "core": up(ic, j, n_core)}
        send("nz", ("nz",), nz.at[0], nz.at[slot], device)
    arrived(("nz",), nz.at[pl.ds(1, len(line))])
    square_sum = jnp.sum(jnp.sum(nz[...], axis=0), axis=1, keepdims=True)
    limit = 0.5 * math.sqrt(entries)
    factor = jnp.minimum(1.0, limit / jnp.sqrt(square_sum + 1e-06))

    def update(h):
        at = cols(h)
        clipped = factor * tf[h, 3]
        new_first = 0.9 * state[1, :, at] + 0.1 * clipped
        new_second = 0.95 * state[2, :, at] + 0.05 * clipped * clipped
        first_hat = new_first * (1.0 / first_bias)
        second_hat = new_second * (1.0 / second_bias)
        master = state[0, :, at]
        new_master = master - 0.01 * (
            first_hat / (jnp.sqrt(second_hat) + 1e-08) + 0.1 * master
        )
        params[iy, ix, :, at] = new_master.astype(BF16)
        w_out[:, at] = new_master
        m_out[:, at] = new_first
        v_out[:, at] = new_second

    def piece(h, ai, bi, side):
        y, x = block(h, ai, bi)
        return params.at[y, x, :, cols(h, side)]

    arrived_from = (0, 3, 1, 2)

    def gather_second(relayed, halves):
        for h in halves:
            for direction in range(2):
                side = direction if relayed else 1 - direction
                part = piece(h, a[h], b[h], side)
                send("ag", ("g2", h, direction, side), part, part, along_second(h, direction))

    def forward_second(direction):
        for h in range(2):
            arrived(("g2", h, direction, direction), x2.at[0, 0])
            part = piece(h, a[h], up(b[h], step_of[1 - direction]), direction)
            send("ag", ("f2", h, direction), part, part, along_second(h, direction))

    def gather_first(j, side):
        for h in range(2):
            if j in (1, 2):
                if side != j - 1:
                    arrived(("g2", h, j - 1, side), x2.at[0, 0])
            if j == 3:
                arrived(("f2", h, side), x2.at[0, 0])
            part = piece(h, a[h], up(b[h], arrived_from[j]), side)
            for direction in range(2):
                send("ag", ("g1", h, j, side), part, part, along_first(h, direction))

    def forward_first(j, direction):
        for h in range(2):
            arrived(("g1", h, j, direction), x2.at[0])
            came_from = up(a[h], step_of[1 - direction])
            part = piece(h, came_from, up(b[h], arrived_from[j]), direction)
            send("ag", ("f1",), part, part, along_first(h, direction))

    for h in range(2):
        update(h)
        gather_second(True, (h,))
    gather_first(0, 0)
    gather_first(0, 1)
    gather_second(False, (0, 1))
    forward_second(0)
    gather_first(1, 0)
    forward_second(1)
    gather_first(2, 1)
    gather_first(1, 1)
    gather_first(3, 0)
    gather_first(2, 0)
    forward_first(1, 0)
    gather_first(3, 1)
    forward_first(0, 1)
    forward_first(0, 0)
    forward_first(1, 1)
    forward_first(2, 0)
    forward_first(2, 1)
    forward_first(3, 0)
    forward_first(3, 1)
    all_sent("rs", land)
    all_sent("np", np_.at[pl.ds(1, 15)])
    all_sent("nz", nz.at[pl.ds(1, len(line))])
    arrived(("f1",), x1)
    all_sent("ag", land)


def write_out(*refs):
    n = (len(refs) - 1) // 2
    sources, targets, sems = refs[:n], refs[n : 2 * n], refs[-1]
    copies = []
    for src, dst in zip(sources, targets):
        parts = [(src.at[i], dst.at[i]) for i in range(4)] if len(src.shape) == 4 else [(src, dst)]
        copies += parts
    made = [
        pltpu.make_async_copy(src, dst, sems.at[i]) for i, (src, dst) in enumerate(copies)
    ]
    for copy in made:
        copy.start()
    for copy in made:
        copy.wait()


def per_device(gradients, master_weights, first_moment, second_moment):
    rows, width = master_weights.shape
    entries = rows * lax.axis_size(DP) * lax.axis_size(SHARD) * width
    half, quarter = width // 2, width // 4
    grads = gradients.reshape(4, 4, rows, width)
    shapes = [((4, 4, rows, width), BF16)] + [((rows, width), F32)] * 3
    hbm = pl.BlockSpec(memory_space=pltpu.HBM)
    vmem = pl.BlockSpec(memory_space=pltpu.VMEM)
    z_size = lax.axis_size("z")
    results = pl.pallas_call(
        lambda *refs: kernel(entries, *refs),
        out_shape=[pltpu.VMEM(*shape) for shape in shapes],
        in_specs=[hbm] * 4,
        out_specs=[vmem] * 4,
        scratch_shapes=[
            pltpu.VMEM((2, 4, rows, half), BF16),
            pltpu.VMEM((2, 4, 4, rows, half), BF16),
            pltpu.VMEM((60, rows, quarter), BF16),
            pltpu.VMEM((2, 4, 2, rows, quarter), BF16),
            pltpu.VMEM((2, 4, rows, half), F32),
            pltpu.VMEM((2, 3, rows, half), BF16),
            pltpu.VMEM((2, 2, rows, quarter), BF16),
            pltpu.VMEM((3, rows, width), F32),
            pltpu.VMEM((16, 1, 128), F32),
            pltpu.VMEM((z_size * lax.axis_size("core"), 1, 128), F32),
            pltpu.SemaphoreType.DMA((len(LOADED),)),
            pltpu.SemaphoreType.DMA((len(SENT),)),
            pltpu.SemaphoreType.DMA((len(RECEIVED),)),
            pltpu.SemaphoreType.REGULAR((z_size // 2,)),
        ],
        compiler_params=pltpu.CompilerParams(
            collective_id=0, has_side_effects=True, vmem_limit_bytes=VMEM_LIMIT
        ),
    )(grads, master_weights, first_moment, second_moment)
    parameters, new_master, new_first, new_second = pl.pallas_call(
        write_out,
        out_shape=[jax.ShapeDtypeStruct(*shape) for shape in shapes],
        in_specs=[vmem] * 4,
        out_specs=[hbm] * 4,
        scratch_shapes=[pltpu.SemaphoreType.DMA((7,))],
        compiler_params=pltpu.CompilerParams(vmem_limit_bytes=2**20),
    )(*results)
    return (parameters.reshape(16 * rows, width), new_master, new_first, new_second)


def solution(mesh):
    split = Mesh(mesh.devices.reshape(4, 4, 8, 2), ("y", "x", "z", "core"))
    return jax.shard_map(
        per_device,
        mesh=split,
        in_specs=(P(DP, SHARD, None), P(SHARD_DP, None), P(SHARD_DP, None), P(SHARD_DP, None)),
        out_specs=(P(SHARD, None), P(SHARD_DP, None), P(SHARD_DP, None), P(SHARD_DP, None)),
        check_vma=False,
    )
```

time: 125 us -> 58.3 us (0.47); the launches traced: 123 us -> 58.2 us
  blocking collectives: 115 us -> 0 us
  Pallas kernels: 0 us -> 57.6 us
  other arithmetic: 3.77 us -> 0 us
  local copies, waits for them, and re-layouts: 3.36 us -> 0 us
    all_to_all x4 -> x0, blocking collectives: 115 us -> none  [the longest x3 68.4 us: sent_to_all(): lax.all_to_all(jnp.broadcast_to(array[None], (size, *array.shape)), axis,...]
    pallas_call x0 -> x2, Pallas kernels: none -> 57.6 us  [the longest x1 55.5 us: per_device(): pl.pallas_call(lambda *refs: kernel(entries, *refs), out_shape=[pltpu.VME...]
    reduce_sum x4 -> x0, other arithmetic: 2.57 us -> none  [the longest x2 1.27 us: of_everyone(): return jnp.sum(everything, axis=0)]
    broadcast_in_dim x3 -> x0, local copies, waits for them, and re-layouts: 1.68 us -> none  [sent_to_all(): jnp.broadcast_to(array[None], (size, *array.shape))]
    unnamed x7 -> x0, local copies, waits for them, and re-layouts: 1.68 us -> none
where the time goes in v3:
time: 58.3 us; the launch traced here: 58.2 us
  Pallas kernels  57.6 us (99%)
  between operations  0.64 us (1%)
    pallas_call x1, Pallas kernels, per_device(): pl.pallas_call(lambda *refs: kernel(entries, *refs), out_shape=[pltpu.VME...  55.5 us
    pallas_call x1, Pallas kernels, per_device(): pl.pallas_call(write_out, out_shape=[jax.ShapeDtypeStruct(*shape) for sha...  2.1 us

profile of v3, /device:TPU:1, one launch (start us, length us, event | category | flops | bytes accessed | tf_op | source)
XLA Modules:
  0.0 58.2 jit_solution(11480190678516135690)
XLA Ops:
  0.6 55.5 %shard_map.75 = (bf16[4,4,48,2048]{3,2,1,0:T(8,128)(2,1)S(1)}, f32[48,2048]{1,0:T(8,128)S(1)}, f32[48,2048]{1,0:T(8,128)S(1)}, f32[48,2048]{1,0:T(8,128)S(1)}) custom-call(bf16[4,4,48,2048]{3,2,1,0:T(8,128)(2,1)} %bitcast.2, f32[48,2048]{1,0:T(8,128)} %refs_1_.1, f32[48,2048]{1,0:T(8,128)} %refs_2_.1, f32[48,2048]{1,0:T(8,128)} %refs_3_.1), custom_call_target="tpu_custom_call" | custom-call | tf_op jit(solution)/shard_map/pallas_call | solution.py:405
  56.1 2.1 %shard_map.76 = (bf16[4,4,48,2048]{3,2,1,0:T(8,128)(2,1)}, f32[48,2048]{1,0:T(8,128)}, f32[48,2048]{1,0:T(8,128)}, f32[48,2048]{1,0:T(8,128)}) custom-call(bf16[4,4,48,2048]{3,2,1,0:T(8,128)(2,1)S(1)} %get-tuple-element.12.refs_0_, f32[48,2048]{1,0:T(8,128)S(1)} %get-tuple-element.13.refs_1_, f32[48,2048]{1,0:T(8,128)S(1)} %get-tuple-element.14.refs_2_, ...), custom_call_target="tpu_custom_call" | custom-call | tf_op jit(solution)/shard_map/pallas_call | solution.py:430

commit v4 on v3

--- a/solution.py
+++ b/solution.py
@@ -31,12 +31,13 @@
     return {key: at for at, key in enumerate(keys)}
 
 
-RECEIVED = table(
-    ("r1", 2, 4), ("d1", 2, 4), ("r2", 2), ("d2", 2), ("np",), ("nz",),
-    ("g2", 2, 2, 2), ("f2", 2, 2), ("g1", 2, 4, 2), ("f1",),
-)
+NORM = table(("np",), ("nz",))
+REDUCE = table(*NORM, ("r1", 4), ("d1", 4), ("r2",), ("d2",))
+GATHER = table(*NORM, ("g2", 2, 2), ("f2", 2), ("g1", 4, 2), ("f1",))
+RECEIVED = {**REDUCE, **GATHER}
+N_RECEIVED = max(len(REDUCE), len(GATHER))
 SENT = table(("rs",), ("np",), ("nz",), ("ag",))
-LOADED = table(("gx", 2), ("gv", 2), ("state",))
+LOADED = table(("gx",), ("gv",), ("state",))
 
 
 def kernel(
@@ -63,10 +64,10 @@
     group_by = (2, 1, 3, 0)
 
     def r1(h, k):
-        return land.at[pl.ds((h * 4 + k) * 2, 2)]
+        return land.at[pl.ds((k * 2 + h) * 2, 2)]
 
     def d1(h, k):
-        return land.at[pl.ds(16 + (h * 4 + k) * 4, 4)]
+        return land.at[pl.ds(16 + (k * 2 + h) * 4, 4)]
 
     def r2(h):
         return land.at[pl.ds(48 + h * 2, 2)]
@@ -108,7 +109,7 @@
     for h in range(2):
         far = up(a[h], 2)
         src = g_hbm.at[:, far, :, cols(h)] if h == 0 else g_hbm.at[far, :, :, cols(h)]
-        load(("gx", h), src, gx.at[h])
+        load(("gx",), src, gx.at[h])
 
     barrier = pltpu.get_barrier_semaphore()
     neighbours = [{"x": up(ix, s)} for s in step_of] + [{"y": up(iy, s)} for s in step_of]
@@ -118,7 +119,7 @@
         pl.semaphore_signal(barrier, inc=1, device_id=device, device_id_type=MESH)
 
     for h in range(2):
-        load(("gv", h), g_hbm.at[:, :, :, cols(h)], gv.at[h])
+        load(("gv",), g_hbm.at[:, :, :, cols(h)], gv.at[h])
     for i, ref in enumerate((w_hbm, m_hbm, v_hbm)):
         load(("state",), ref, state.at[i])
     pl.semaphore_wait(barrier, len(neighbours))
@@ -154,7 +155,7 @@
             bi = up(b[h], group_by[k])
             for direction in range(2):
                 send(
-                    "rs", ("r1", h, k),
+                    "rs", ("r1", k),
                     gx.at[h, bi, :, side_cols(direction)],
                     r1(h, k).at[direction],
                     along_first(h, direction),
@@ -167,16 +168,16 @@
                 other = 1 - direction
                 y, x = block(h, up(a[h], step_of[direction]), bi)
                 send(
-                    "rs", ("d1", h, k),
+                    "rs", ("d1", k),
                     gv.at[h, y, x, :, side_cols(other)],
                     d1(h, k).at[direction * 2 + other],
                     along_first(h, direction),
                 )
 
     def relay(k):
+        arrived(("r1", k), land.at[pl.ds(k * 4, 4)])
         for h in range(2):
             bi = up(b[h], group_by[k])
-            arrived(("r1", h, k), r1(h, k))
             for direction in range(2):
                 y, x = block(h, up(a[h], step_of[direction]), bi)
                 x1[h, k, direction] = (
@@ -184,16 +185,16 @@
                     + r1(h, k)[direction].astype(F32)
                 ).astype(BF16)
                 send(
-                    "rs", ("d1", h, k),
+                    "rs", ("d1", k),
                     x1.at[h, k, direction],
                     d1(h, k).at[direction * 2 + direction],
                     along_first(h, direction),
                 )
 
     def complete(k):
+        arrived(("d1", k), land.at[pl.ds(16 + k * 8, 8)])
         for h in range(2):
             bi = up(b[h], group_by[k])
-            arrived(("d1", h, k), d1(h, k))
             y, x = block(h, a[h], bi)
             total = gv[h, y, x].astype(F32) + whole(d1(h, k), 0) + whole(d1(h, k), 1)
             tf[h, k] = total
@@ -202,7 +203,7 @@
             if k == 0:
                 for direction in range(2):
                     send(
-                        "rs", ("r2", h),
+                        "rs", ("r2",),
                         tb.at[h, 0, :, side_cols(direction)],
                         r2(h).at[direction],
                         along_second(h, direction),
@@ -211,34 +212,32 @@
                 direction = k - 1
                 other = 1 - direction
                 send(
-                    "rs", ("d2", h),
+                    "rs", ("d2",),
                     tb.at[h, k, :, side_cols(other)],
                     d2(h).at[direction * 2 + other],
                     along_second(h, direction),
                 )
 
     def relay_second():
-        for h in range(2):
-            arrived(("r2", h), r2(h))
+        arrived(("r2",), land.at[pl.ds(48, 4)])
+        for h in range(2):
             for direction in range(2):
                 x2[h, direction] = (
                     tf[h, 1 + direction, :, side_cols(direction)]
                     + r2(h)[direction].astype(F32)
                 ).astype(BF16)
                 send(
-                    "rs", ("d2", h),
+                    "rs", ("d2",),
                     x2.at[h, direction],
                     d2(h).at[direction * 2 + direction],
                     along_second(h, direction),
                 )
 
-    for h in range(2):
-        loaded(("gx", h), gx.at[h])
+    loaded(("gx",), gx)
     for k in range(4):
         send_far(k)
     tell(0)
-    for h in range(2):
-        loaded(("gv", h), gv.at[h])
+    loaded(("gv",), gv)
     send_near(0)
     relay(0)
     told(0)
@@ -262,8 +261,8 @@
     loaded(("state",), state)
 
     lanes = jnp.zeros((8, 128), F32)
+    arrived(("d2",), land.at[pl.ds(52, 8)])
     for h in range(2):
-        arrived(("d2", h), d2(h))
         total = tf[h, 3] + whole(d2(h), 0) + whole(d2(h), 1)
         tf[h, 3] = total
         square = total * total
@@ -295,9 +294,9 @@
     limit = 0.5 * math.sqrt(entries)
     factor = jnp.minimum(1.0, limit / jnp.sqrt(square_sum + 1e-06))
 
-    def update(h):
-        at = cols(h)
-        clipped = factor * tf[h, 3]
+    def update(h, side):
+        at = cols(h, side)
+        clipped = factor * tf[h, 3, :, side_cols(side)]
         new_first = 0.9 * state[1, :, at] + 0.1 * clipped
         new_second = 0.95 * state[2, :, at] + 0.05 * clipped * clipped
         first_hat = new_first * (1.0 / first_bias)
@@ -317,43 +316,44 @@
 
     arrived_from = (0, 3, 1, 2)
 
-    def gather_second(relayed, halves):
-        for h in halves:
-            for direction in range(2):
-                side = direction if relayed else 1 - direction
-                part = piece(h, a[h], b[h], side)
-                send("ag", ("g2", h, direction, side), part, part, along_second(h, direction))
+    two, four = x2.at[0], x2
+
+    def gather_second(h, direction, side):
+        part = piece(h, a[h], b[h], side)
+        send("ag", ("g2", direction, side), part, part, along_second(h, direction))
 
     def forward_second(direction):
-        for h in range(2):
-            arrived(("g2", h, direction, direction), x2.at[0, 0])
+        arrived(("g2", direction, direction), two)
+        for h in range(2):
             part = piece(h, a[h], up(b[h], step_of[1 - direction]), direction)
-            send("ag", ("f2", h, direction), part, part, along_second(h, direction))
+            send("ag", ("f2", direction), part, part, along_second(h, direction))
 
     def gather_first(j, side):
-        for h in range(2):
-            if j in (1, 2):
-                if side != j - 1:
-                    arrived(("g2", h, j - 1, side), x2.at[0, 0])
-            if j == 3:
-                arrived(("f2", h, side), x2.at[0, 0])
+        if j in (1, 2) and side != j - 1:
+            arrived(("g2", j - 1, side), two)
+        if j == 3:
+            arrived(("f2", side), two)
+        for h in range(2):
             part = piece(h, a[h], up(b[h], arrived_from[j]), side)
             for direction in range(2):
-                send("ag", ("g1", h, j, side), part, part, along_first(h, direction))
+                send("ag", ("g1", j, side), part, part, along_first(h, direction))
 
     def forward_first(j, direction):
-        for h in range(2):
-            arrived(("g1", h, j, direction), x2.at[0])
+        arrived(("g1", j, direction), four)
+        for h in range(2):
             came_from = up(a[h], step_of[1 - direction])
             part = piece(h, came_from, up(b[h], arrived_from[j]), direction)
             send("ag", ("f1",), part, part, along_first(h, direction))
 
-    for h in range(2):
-        update(h)
-        gather_second(True, (h,))
+    for direction in range(2):
+        for h in range(2):
+            update(h, direction)
+            gather_second(h, direction, direction)
     gather_first(0, 0)
     gather_first(0, 1)
-    gather_second(False, (0, 1))
+    for h in range(2):
+        for direction in range(2):
+            gather_second(h, direction, 1 - direction)
     forward_second(0)
     gather_first(1, 0)
     forward_second(1)
@@ -420,7 +420,7 @@
             pltpu.VMEM((z_size * lax.axis_size("core"), 1, 128), F32),
             pltpu.SemaphoreType.DMA((len(LOADED),)),
             pltpu.SemaphoreType.DMA((len(SENT),)),
-            pltpu.SemaphoreType.DMA((len(RECEIVED),)),
+            pltpu.SemaphoreType.DMA((N_RECEIVED,)),
             pltpu.SemaphoreType.REGULAR((z_size // 2,)),
         ],
         compiler_params=pltpu.CompilerParams(

time: 58.3 us -> 57.8 us (level)
  Pallas kernels: 57.6 us -> 56.9 us
    pallas_call x1, Pallas kernels: 55.5 us -> 54.8 us  [per_device(): pl.pallas_call(lambda *refs: kernel(entries, *refs), out_shape=[pltpu.VME...]
where the time goes in v4:
time: 57.8 us; the launch traced here: 57.6 us
  Pallas kernels  56.9 us (98%)
  between operations  0.64 us (1%)
    pallas_call x1, Pallas kernels, per_device(): pl.pallas_call(lambda *refs: kernel(entries, *refs), out_shape=[pltpu.VME...  54.8 us
    pallas_call x1, Pallas kernels, per_device(): pl.pallas_call(write_out, out_shape=[jax.ShapeDtypeStruct(*shape) for sha...  2.1 us

profile of v4, /device:TPU:1, one launch (start us, length us, event | category | flops | bytes accessed | tf_op | source)
XLA Modules:
  0.0 57.6 jit_solution(18100351682644063393)
XLA Ops:
  0.6 54.8 %shard_map.75 = (bf16[4,4,48,2048]{3,2,1,0:T(8,128)(2,1)S(1)}, f32[48,2048]{1,0:T(8,128)S(1)}, f32[48,2048]{1,0:T(8,128)S(1)}, f32[48,2048]{1,0:T(8,128)S(1)}) custom-call(bf16[4,4,48,2048]{3,2,1,0:T(8,128)(2,1)} %bitcast.2, f32[48,2048]{1,0:T(8,128)} %refs_1_.1, f32[48,2048]{1,0:T(8,128)} %refs_2_.1, f32[48,2048]{1,0:T(8,128)} %refs_3_.1), custom_call_target="tpu_custom_call" | custom-call | tf_op jit(solution)/shard_map/pallas_call | solution.py:405
  55.5 2.1 %shard_map.76 = (bf16[4,4,48,2048]{3,2,1,0:T(8,128)(2,1)}, f32[48,2048]{1,0:T(8,128)}, f32[48,2048]{1,0:T(8,128)}, f32[48,2048]{1,0:T(8,128)}) custom-call(bf16[4,4,48,2048]{3,2,1,0:T(8,128)(2,1)S(1)} %get-tuple-element.12.refs_0_, f32[48,2048]{1,0:T(8,128)S(1)} %get-tuple-element.13.refs_1_, f32[48,2048]{1,0:T(8,128)S(1)} %get-tuple-element.14.refs_2_, ...), custom_call_target="tpu_custom_call" | custom-call | tf_op jit(solution)/shard_map/pallas_call | solution.py:430

commit v5 on v4

--- a/solution.py
+++ b/solution.py
@@ -31,12 +31,12 @@
     return {key: at for at, key in enumerate(keys)}
 
 
-NORM = table(("np",), ("nz",))
+NORM = table(("norm",))
 REDUCE = table(*NORM, ("r1", 4), ("d1", 4), ("r2",), ("d2",))
 GATHER = table(*NORM, ("g2", 2, 2), ("f2", 2), ("g1", 4, 2), ("f1",))
 RECEIVED = {**REDUCE, **GATHER}
 N_RECEIVED = max(len(REDUCE), len(GATHER))
-SENT = table(("rs",), ("np",), ("nz",), ("ag",))
+SENT = table(("rs",), ("norm",), ("ag",))
 LOADED = table(("gx",), ("gv",), ("state",))
 
 
@@ -44,7 +44,7 @@
     entries,
     g_hbm, w_hbm, m_hbm, v_hbm,
     params, w_out, m_out, v_out,
-    gx, gv, land, x1, tf, tb, x2, state, np_, nz,
+    gx, gv, land, x1, tf, tb, x2, state, parts,
     load_sems, send_sems, recv_sems, gossip,
 ):
     ix, iy = lax.axis_index("x"), lax.axis_index("y")
@@ -124,15 +124,20 @@
         load(("state",), ref, state.at[i])
     pl.semaphore_wait(barrier, len(neighbours))
 
+    links = {
+        "x": [{"x": up(ix, s)} for s in step_of],
+        "core": [{"core": up(ic, s, n_core)} for s in range(1, n_core)],
+        "y": [{"y": up(iy, s)} for s in step_of],
+        "z": [{"z": up(iz, s, z_size)} for s in (1, z_size - 1)],
+    }
+    rounds = ["x", "core", "y", "y"] + ["z"] * (z_size // 2)
+
     def tell(r):
-        for s in (1, z_size - 1):
-            pl.semaphore_signal(
-                gossip.at[r], inc=1,
-                device_id={"z": up(iz, s, z_size)}, device_id_type=MESH,
-            )
+        for device in links[rounds[r]]:
+            pl.semaphore_signal(gossip.at[r], inc=1, device_id=device, device_id_type=MESH)
 
     def told(r):
-        pl.semaphore_wait(gossip.at[r], 2)
+        pl.semaphore_wait(gossip.at[r], len(links[rounds[r]]))
 
     def send(sent, key, src, dst, device):
         pltpu.make_async_remote_copy(
@@ -239,25 +244,36 @@
     tell(0)
     loaded(("gv",), gv)
     send_near(0)
-    relay(0)
     told(0)
     tell(1)
+    told(1)
+    tell(2)
+    told(2)
+    tell(3)
+    relay(0)
     send_near(1)
+    told(3)
+    tell(4)
     relay(1)
     relay(2)
-    told(1)
-    tell(2)
+    told(4)
+    tell(5)
     send_near(2)
     complete(0)
+    told(5)
+    tell(6)
     relay(3)
-    told(2)
-    tell(3)
     complete(1)
+    told(6)
+    tell(7)
     send_near(3)
     complete(2)
     relay_second()
     complete(3)
-    told(3)
+    for r in range(7, len(rounds)):
+        told(r)
+        if r + 1 < len(rounds):
+            tell(r + 1)
     loaded(("state",), state)
 
     lanes = jnp.zeros((8, 128), F32)
@@ -270,27 +286,30 @@
         for c in range(half // 128):
             lanes = lanes + by_row[:, c * 128 : (c + 1) * 128]
 
-    np_[0] = jnp.sum(lanes, axis=0, keepdims=True)
-    distance = {0: 0, 1: 1, 2: 2, 3: 1}
-    plane = sorted(
-        ((i, j) for i in range(4) for j in range(4)),
-        key=lambda at: -distance[at[0]] - distance[at[1]],
-    )[:-1]
-    for i, j in plane:
-        slot = i * 4 + j
-        send("np", ("np",), np_.at[0], np_.at[slot], {"y": up(iy, i), "x": up(ix, j)})
-    arrived(("np",), np_.at[pl.ds(1, 15)])
-    nz[0] = jnp.sum(np_[...], axis=0)
-    line = sorted(
-        ((i, j) for i in range(z_size) for j in range(n_core)),
-        key=lambda at: -min(at[0], z_size - at[0]) - 0.5 * at[1],
-    )[:-1]
-    for i, j in line:
-        slot = i * n_core + j
-        device = {"z": up(iz, i, z_size), "core": up(ic, j, n_core)}
-        send("nz", ("nz",), nz.at[0], nz.at[slot], device)
-    arrived(("nz",), nz.at[pl.ds(1, len(line))])
-    square_sum = jnp.sum(jnp.sum(nz[...], axis=0), axis=1, keepdims=True)
+    me = ((iz * n_core + ic) * 4 + iy) * 4 + ix
+    parts[me] = jnp.sum(lanes, axis=0, keepdims=True)
+
+    def tell_part(device):
+        send("norm", ("norm",), parts.at[me], parts.at[me], device)
+
+    def tell_row(z, i):
+        for x in range(4):
+            tell_part({"z": z, "core": i // 4, "y": lax.rem(i, 4), "x": x})
+
+    for z in (0, 1, 2, 3, 7, 4, 5, 6):
+        @pl.when(z != iz)
+        def _():
+            lax.fori_loop(0, 4 * n_core, lambda i, c: (tell_row(z, i), c)[1], 0)
+
+    for i in range(n_core):
+        for y in range(4):
+            for x in range(4):
+                if (i, y, x) != (0, 0, 0):
+                    tell_part({"core": up(ic, i, n_core), "y": up(iy, y), "x": up(ix, x)})
+
+    n_all = 16 * z_size * n_core
+    arrived(("norm",), parts.at[pl.ds(0, n_all - 1)])
+    square_sum = jnp.sum(jnp.sum(parts[...], axis=0), axis=1, keepdims=True)
     limit = 0.5 * math.sqrt(entries)
     factor = jnp.minimum(1.0, limit / jnp.sqrt(square_sum + 1e-06))
 
@@ -371,8 +390,7 @@
     forward_first(3, 0)
     forward_first(3, 1)
     all_sent("rs", land)
-    all_sent("np", np_.at[pl.ds(1, 15)])
-    all_sent("nz", nz.at[pl.ds(1, len(line))])
+    all_sent("norm", parts.at[pl.ds(0, n_all - 1)])
     arrived(("f1",), x1)
     all_sent("ag", land)
 
@@ -416,12 +434,11 @@
             pltpu.VMEM((2, 3, rows, half), BF16),
             pltpu.VMEM((2, 2, rows, quarter), BF16),
             pltpu.VMEM((3, rows, width), F32),
-            pltpu.VMEM((16, 1, 128), F32),
-            pltpu.VMEM((z_size * lax.axis_size("core"), 1, 128), F32),
+            pltpu.VMEM((16 * z_size * lax.axis_size("core"), 1, 128), F32),
             pltpu.SemaphoreType.DMA((len(LOADED),)),
             pltpu.SemaphoreType.DMA((len(SENT),)),
             pltpu.SemaphoreType.DMA((N_RECEIVED,)),
-            pltpu.SemaphoreType.REGULAR((z_size // 2,)),
+            pltpu.SemaphoreType.REGULAR((4 + z_size // 2,)),
         ],
         compiler_params=pltpu.CompilerParams(
             collective_id=0, has_side_effects=True, vmem_limit_bytes=VMEM_LIMIT

time: 57.8 us -> 56.2 us (0.972)
  Pallas kernels: 56.9 us -> 55.5 us
    pallas_call x1, Pallas kernels: 54.8 us -> 53.4 us  [per_device(): pl.pallas_call(lambda *refs: kernel(entries, *refs), out_shape=[pltpu.VME...]
where the time goes in v5:
time: 56.2 us
  Pallas kernels  55.5 us (99%)
  between operations  0.64 us (1%)
    pallas_call x1, Pallas kernels, per_device(): pl.pallas_call(lambda *refs: kernel(entries, *refs), out_shape=[pltpu.VME...  53.4 us
    pallas_call x1, Pallas kernels, per_device(): pl.pallas_call(write_out, out_shape=[jax.ShapeDtypeStruct(*shape) for sha...  2.1 us

profile of v5, /device:TPU:1, one launch (start us, length us, event | category | flops | bytes accessed | tf_op | source)
XLA Modules:
  0.0 56.2 jit_solution(6869634909301564308)
XLA Ops:
  0.6 53.4 %shard_map.75 = (bf16[4,4,48,2048]{3,2,1,0:T(8,128)(2,1)S(1)}, f32[48,2048]{1,0:T(8,128)S(1)}, f32[48,2048]{1,0:T(8,128)S(1)}, f32[48,2048]{1,0:T(8,128)S(1)}) custom-call(bf16[4,4,48,2048]{3,2,1,0:T(8,128)(2,1)} %bitcast.2, f32[48,2048]{1,0:T(8,128)} %refs_1_.1, f32[48,2048]{1,0:T(8,128)} %refs_2_.1, f32[48,2048]{1,0:T(8,128)} %refs_3_.1), custom_call_target="tpu_custom_call" | custom-call | tf_op jit(solution)/shard_map/pallas_call | solution.py:423
  54.1 2.1 %shard_map.76 = (bf16[4,4,48,2048]{3,2,1,0:T(8,128)(2,1)}, f32[48,2048]{1,0:T(8,128)}, f32[48,2048]{1,0:T(8,128)}, f32[48,2048]{1,0:T(8,128)}) custom-call(bf16[4,4,48,2048]{3,2,1,0:T(8,128)(2,1)S(1)} %get-tuple-element.12.refs_0_, f32[48,2048]{1,0:T(8,128)S(1)} %get-tuple-element.13.refs_1_, f32[48,2048]{1,0:T(8,128)S(1)} %get-tuple-element.14.refs_2_, ...), custom_call_target="tpu_custom_call" | custom-call | tf_op jit(solution)/shard_map/pallas_call | solution.py:447

commit v6 on v5

--- a/solution.py
+++ b/solution.py
@@ -106,11 +106,6 @@
     def loaded(key, dst):
         pltpu.make_async_copy(dst, dst, load_sems.at[LOADED[key]]).wait()
 
-    for h in range(2):
-        far = up(a[h], 2)
-        src = g_hbm.at[:, far, :, cols(h)] if h == 0 else g_hbm.at[far, :, :, cols(h)]
-        load(("gx",), src, gx.at[h])
-
     barrier = pltpu.get_barrier_semaphore()
     neighbours = [{"x": up(ix, s)} for s in step_of] + [{"y": up(iy, s)} for s in step_of]
     neighbours += [{"z": up(iz, s, z_size)} for s in (1, z_size - 1)]
@@ -118,6 +113,10 @@
     for device in neighbours:
         pl.semaphore_signal(barrier, inc=1, device_id=device, device_id_type=MESH)
 
+    for h in range(2):
+        far = up(a[h], 2)
+        src = g_hbm.at[:, far, :, cols(h)] if h == 0 else g_hbm.at[far, :, :, cols(h)]
+        load(("gx",), src, gx.at[h])
     for h in range(2):
         load(("gv",), g_hbm.at[:, :, :, cols(h)], gv.at[h])
     for i, ref in enumerate((w_hbm, m_hbm, v_hbm)):
@@ -309,7 +308,10 @@
 
     n_all = 16 * z_size * n_core
     arrived(("norm",), parts.at[pl.ds(0, n_all - 1)])
-    square_sum = jnp.sum(jnp.sum(parts[...], axis=0), axis=1, keepdims=True)
+    rest = [parts[i] for i in range(n_all)]
+    while len(rest) > 1:
+        rest = [p + q for p, q in zip(rest[::2], rest[1::2])]
+    square_sum = jnp.sum(rest[0], axis=1, keepdims=True)
     limit = 0.5 * math.sqrt(entries)
     factor = jnp.minimum(1.0, limit / jnp.sqrt(square_sum + 1e-06))
 

time: 56.2 us -> 56 us (level)
  no operation moved by 1% of the time
where the time goes in v6:
time: 56 us; the launch traced here: 55.9 us
  Pallas kernels  55.3 us (99%)
  between operations  0.64 us (1%)
    pallas_call x1, Pallas kernels, per_device(): pl.pallas_call(lambda *refs: kernel(entries, *refs), out_shape=[pltpu.VME...  53.2 us
    pallas_call x1, Pallas kernels, per_device(): pl.pallas_call(write_out, out_shape=[jax.ShapeDtypeStruct(*shape) for sha...  2.1 us

profile of v6, /device:TPU:1, one launch (start us, length us, event | category | flops | bytes accessed | tf_op | source)
XLA Modules:
  0.0 55.9 jit_solution(13700486692548633828)
XLA Ops:
  0.6 53.2 %shard_map.75 = (bf16[4,4,48,2048]{3,2,1,0:T(8,128)(2,1)S(1)}, f32[48,2048]{1,0:T(8,128)S(1)}, f32[48,2048]{1,0:T(8,128)S(1)}, f32[48,2048]{1,0:T(8,128)S(1)}) custom-call(bf16[4,4,48,2048]{3,2,1,0:T(8,128)(2,1)} %bitcast.2, f32[48,2048]{1,0:T(8,128)} %refs_1_.1, f32[48,2048]{1,0:T(8,128)} %refs_2_.1, f32[48,2048]{1,0:T(8,128)} %refs_3_.1), custom_call_target="tpu_custom_call" | custom-call | tf_op jit(solution)/shard_map/pallas_call | solution.py:425
  53.8 2.1 %shard_map.76 = (bf16[4,4,48,2048]{3,2,1,0:T(8,128)(2,1)}, f32[48,2048]{1,0:T(8,128)}, f32[48,2048]{1,0:T(8,128)}, f32[48,2048]{1,0:T(8,128)}) custom-call(bf16[4,4,48,2048]{3,2,1,0:T(8,128)(2,1)S(1)} %get-tuple-element.12.refs_0_, f32[48,2048]{1,0:T(8,128)S(1)} %get-tuple-element.13.refs_1_, f32[48,2048]{1,0:T(8,128)S(1)} %get-tuple-element.14.refs_2_, ...), custom_call_target="tpu_custom_call" | custom-call | tf_op jit(solution)/shard_map/pallas_call | solution.py:449

commit v7 on v6

--- a/solution.py
+++ b/solution.py
@@ -293,12 +293,13 @@
 
     def tell_row(z, i):
         for x in range(4):
-            tell_part({"z": z, "core": i // 4, "y": lax.rem(i, 4), "x": x})
+            tell_part({"z": z, "core": i // 4, "y": i % 4, "x": x})
 
     for z in (0, 1, 2, 3, 7, 4, 5, 6):
         @pl.when(z != iz)
         def _():
-            lax.fori_loop(0, 4 * n_core, lambda i, c: (tell_row(z, i), c)[1], 0)
+            for i in range(4 * n_core):
+                tell_row(z, i)
 
     for i in range(n_core):
         for y in range(4):

time: 56 us -> 56 us (level)
  no operation moved by 1% of the time
where the time goes in v7:
time: 56 us; the launch traced here: 55.9 us
  Pallas kernels  55.3 us (99%)
  between operations  0.64 us (1%)
    pallas_call x1, Pallas kernels, per_device(): pl.pallas_call(lambda *refs: kernel(entries, *refs), out_shape=[pltpu.VME...  53.2 us
    pallas_call x1, Pallas kernels, per_device(): pl.pallas_call(write_out, out_shape=[jax.ShapeDtypeStruct(*shape) for sha...  2.1 us

profile of v7, /device:TPU:1, one launch (start us, length us, event | category | flops | bytes accessed | tf_op | source)
XLA Modules:
  0.0 55.9 jit_solution(1163961070019733155)
XLA Ops:
  0.6 53.2 %shard_map.75 = (bf16[4,4,48,2048]{3,2,1,0:T(8,128)(2,1)S(1)}, f32[48,2048]{1,0:T(8,128)S(1)}, f32[48,2048]{1,0:T(8,128)S(1)}, f32[48,2048]{1,0:T(8,128)S(1)}) custom-call(bf16[4,4,48,2048]{3,2,1,0:T(8,128)(2,1)} %bitcast.2, f32[48,2048]{1,0:T(8,128)} %refs_1_.1, f32[48,2048]{1,0:T(8,128)} %refs_2_.1, f32[48,2048]{1,0:T(8,128)} %refs_3_.1), custom_call_target="tpu_custom_call" | custom-call | tf_op jit(solution)/shard_map/pallas_call | solution.py:426
  53.8 2.1 %shard_map.76 = (bf16[4,4,48,2048]{3,2,1,0:T(8,128)(2,1)}, f32[48,2048]{1,0:T(8,128)}, f32[48,2048]{1,0:T(8,128)}, f32[48,2048]{1,0:T(8,128)}) custom-call(bf16[4,4,48,2048]{3,2,1,0:T(8,128)(2,1)S(1)} %get-tuple-element.12.refs_0_, f32[48,2048]{1,0:T(8,128)S(1)} %get-tuple-element.13.refs_1_, f32[48,2048]{1,0:T(8,128)S(1)} %get-tuple-element.14.refs_2_, ...), custom_call_target="tpu_custom_call" | custom-call | tf_op jit(solution)/shard_map/pallas_call | solution.py:450

commit v8 on v7

--- a/solution.py
+++ b/solution.py
@@ -316,7 +316,7 @@
     limit = 0.5 * math.sqrt(entries)
     factor = jnp.minimum(1.0, limit / jnp.sqrt(square_sum + 1e-06))
 
-    def update(h, side):
+    def adam(h, side):
         at = cols(h, side)
         clipped = factor * tf[h, 3, :, side_cols(side)]
         new_first = 0.9 * state[1, :, at] + 0.1 * clipped
@@ -327,10 +327,14 @@
         new_master = master - 0.01 * (
             first_hat / (jnp.sqrt(second_hat) + 1e-08) + 0.1 * master
         )
-        params[iy, ix, :, at] = new_master.astype(BF16)
-        w_out[:, at] = new_master
-        m_out[:, at] = new_first
-        v_out[:, at] = new_second
+        return new_master, new_first, new_second
+
+    def update(h, side):
+        params[iy, ix, :, cols(h, side)] = adam(h, side)[0].astype(BF16)
+
+    def keep(h, side):
+        at = cols(h, side)
+        w_out[:, at], m_out[:, at], v_out[:, at] = adam(h, side)
 
     def piece(h, ai, bi, side):
         y, x = block(h, ai, bi)
@@ -376,6 +380,9 @@
     for h in range(2):
         for direction in range(2):
             gather_second(h, direction, 1 - direction)
+    for h in range(2):
+        for side in range(2):
+            keep(h, side)
     forward_second(0)
     gather_first(1, 0)
     forward_second(1)

time: 56 us -> 56 us (level)
  no operation moved by 1% of the time
where the time goes in v8:
time: 56 us; the launch traced here: 55.9 us
  Pallas kernels  55.3 us (99%)
  between operations  0.64 us (1%)
    pallas_call x1, Pallas kernels, per_device(): pl.pallas_call(lambda *refs: kernel(entries, *refs), out_shape=[pltpu.VME...  53.2 us
    pallas_call x1, Pallas kernels, per_device(): pl.pallas_call(write_out, out_shape=[jax.ShapeDtypeStruct(*shape) for sha...  2.1 us

profile of v8, /device:TPU:1, one launch (start us, length us, event | category | flops | bytes accessed | tf_op | source)
XLA Modules:
  0.0 55.9 jit_solution(335810356408319474)
XLA Ops:
  0.6 53.2 %shard_map.75 = (bf16[4,4,48,2048]{3,2,1,0:T(8,128)(2,1)S(1)}, f32[48,2048]{1,0:T(8,128)S(1)}, f32[48,2048]{1,0:T(8,128)S(1)}, f32[48,2048]{1,0:T(8,128)S(1)}) custom-call(bf16[4,4,48,2048]{3,2,1,0:T(8,128)(2,1)} %bitcast.2, f32[48,2048]{1,0:T(8,128)} %refs_1_.1, f32[48,2048]{1,0:T(8,128)} %refs_2_.1, f32[48,2048]{1,0:T(8,128)} %refs_3_.1), custom_call_target="tpu_custom_call" | custom-call | tf_op jit(solution)/shard_map/pallas_call | solution.py:433
  53.8 2.1 %shard_map.76 = (bf16[4,4,48,2048]{3,2,1,0:T(8,128)(2,1)}, f32[48,2048]{1,0:T(8,128)}, f32[48,2048]{1,0:T(8,128)}, f32[48,2048]{1,0:T(8,128)}) custom-call(bf16[4,4,48,2048]{3,2,1,0:T(8,128)(2,1)S(1)} %get-tuple-element.12.refs_0_, f32[48,2048]{1,0:T(8,128)S(1)} %get-tuple-element.13.refs_1_, f32[48,2048]{1,0:T(8,128)S(1)} %get-tuple-element.14.refs_2_, ...), custom_call_target="tpu_custom_call" | custom-call | tf_op jit(solution)/shard_map/pallas_call | solution.py:457
